TPU v7x, 32 devices: a whole 2x2x4 slice. The times are simulated.
32 devices in a mesh: row: 2 (over y), col: 16 (over z, x, core).
Axes of the slice: x: 2, y: 2, z: 4, core: 2. Of those that a mesh axis runs over, the one named last changes fastest.
Arguments:
- image_student: bfloat16 [2048, 1024], P(('row', 'col')), may hold values from -2.5 to 2.5
- text_student: bfloat16 [2048, 1024], P(('col', 'row')), may hold values from -2.5 to 2.5
- image_teacher: bfloat16 [2048, 1024], P(('row', 'col')), may hold values from -2.5 to 2.5
- text_teacher: bfloat16 [2048, 1024], P(('col', 'row')), may hold values from -2.5 to 2.5
Outputs:
- loss: float32 [], replicated
- image_grad: float32 [2048, 1024], P(('row', 'col'))
- text_grad: float32 [2048, 1024], P(('col', 'row'))
All inputs are finite; a program needn't handle non-finite values.
Results may differ from a plain program's by a relative error of at most 0.002.
Values may be sent and summed in bfloat16 or wider, within the bound.
A program may use at most 128 MiB of HBM per device.

v0:
```python
import jax
import jax.numpy as jnp
from jax import lax
from jax.sharding import PartitionSpec as P

logit_scale = 100.0


def joined(value, axis, join):
    pieces = jax.tree.map(lambda part: lax.all_gather(part, axis), value)
    head = jax.tree.map(lambda part: part[0], pieces)
    tail = jax.tree.map(lambda part: part[1:], pieces)
    subtotal, _ = lax.scan(lambda subtotal, slab: (join(subtotal, slab), None), head, tail)
    return subtotal


def tile_logits(left, right):
    return logit_scale * lax.dot_general(
        left, right, (((1,), (1,)), ((), ())), preferred_element_type=jnp.float32
    )


def partial_stats(student, teacher, along):
    student_high = jnp.max(student, along, keepdims=True)
    student_total = jnp.sum(jnp.exp(student - student_high), along)
    teacher_high = jnp.max(teacher, along, keepdims=True)
    weights = jnp.exp(teacher - teacher_high)
    teacher_total = jnp.sum(weights, along)
    divergence = jnp.sum(weights * (teacher - student), along)
    return (
        jnp.squeeze(student_high, along),
        student_total,
        jnp.squeeze(teacher_high, along),
        teacher_total,
        divergence,
    )


def merge_stats(first, second):
    student_high = jnp.maximum(first[0], second[0])
    teacher_high = jnp.maximum(first[2], second[2])
    early = jnp.exp(first[2] - teacher_high)
    later = jnp.exp(second[2] - teacher_high)
    student_total = first[1] * jnp.exp(first[0] - student_high) + second[1] * jnp.exp(
        second[0] - student_high
    )
    return (
        student_high,
        student_total,
        teacher_high,
        first[3] * early + second[3] * later,
        first[4] * early + second[4] * later,
    )


def finish(stats):
    student_lse = stats[0] + jnp.log(stats[1])
    teacher_lse = stats[2] + jnp.log(stats[3])
    divergence = stats[4] / stats[3] - teacher_lse + student_lse
    return (student_lse, teacher_lse, 0.5 * (student_lse + divergence))


def body(image_student, text_student, image_teacher, text_teacher):
    per_device = image_student.shape[0]
    image_slab, image_frozen = (
        lax.all_gather(image_student, "col", axis=0, tiled=True),
        lax.all_gather(image_teacher, "col", axis=0, tiled=True),
    )
    text_slab, text_frozen = (
        lax.all_gather(text_student, "row", axis=0, tiled=True),
        lax.all_gather(text_teacher, "row", axis=0, tiled=True),
    )
    student = tile_logits(image_slab, text_slab)
    teacher = tile_logits(image_frozen, text_frozen)
    row_stats = joined(partial_stats(student, teacher, 1), "col", merge_stats)
    column_stats = joined(partial_stats(student, teacher, 0), "row", merge_stats)
    student_rows, teacher_rows, row_terms = finish(row_stats)
    student_columns, teacher_columns, column_terms = finish(column_stats)
    row_place = lax.axis_index("row")
    col_place = lax.axis_index("col")
    row_index = row_place * student.shape[0] + jnp.arange(student.shape[0], dtype=jnp.int32)
    column_index = col_place * student.shape[1] + jnp.arange(student.shape[1], dtype=jnp.int32)
    identity = (row_index[:, None] == column_index[None, :]).astype(jnp.float32)
    own_rows = lax.dynamic_slice_in_dim(row_terms, col_place * per_device, per_device)
    own_columns = lax.dynamic_slice_in_dim(column_terms, row_place * per_device, per_device)
    partial_value = jnp.sum(own_rows) + jnp.sum(own_columns) - jnp.sum(student * identity)
    pair_count = per_device * lax.axis_size("row") * lax.axis_size("col")
    loss = lax.psum(partial_value, ("row", "col")) / pair_count
    gradient = (
        jnp.exp(student - student_rows[:, None])
        + jnp.exp(student - student_columns[None, :])
        - 0.5
        * (jnp.exp(teacher - teacher_rows[:, None]) + jnp.exp(teacher - teacher_columns[None, :]))
        - identity
    ).astype(jnp.bfloat16)
    picked = gradient
    image_grad = lax.psum_scatter(
        logit_scale * jnp.dot(picked, text_slab, preferred_element_type=jnp.float32),
        "col",
        scatter_dimension=0,
        tiled=True,
    )
    picked = gradient
    text_grad = lax.psum_scatter(
        logit_scale
        * lax.dot_general(
            picked, image_slab, (((0,), (0,)), ((), ())), preferred_element_type=jnp.float32
        ),
        "row",
        scatter_dimension=0,
        tiled=True,
    )
    return (loss, image_grad, text_grad)


def solution(mesh):
    return jax.shard_map(
        body,
        mesh=mesh,
        in_specs=(
            P(("row", "col"), None),
            P(("col", "row"), None),
            P(("row", "col"), None),
            P(("col", "row"), None),
        ),
        out_specs=(P(), P(("row", "col"), None), P(("col", "row"), None)),
        check_vma=False,
    )
```

profile of v0, /device:TPU:0, one launch (start us, length us, event | category | flops | bytes accessed | tf_op | source)
XLA Modules:
  0.0 348.5 jit_solution(8966833049292975787)
XLA Ops:
  8.7 7.4 %all_gather.61 = bf16[128,1024]{1,0:T(8,128)(2,1)S(1)} all-gather(bf16[64,1024]{1,0:T(8,128)(2,1)} %param.7), channel_id=1, replica_groups=mesh['row'=2,'col'=16] {'row'}, dimensions={0}, use_global_device_ids=true | all-gather | bytes 393216 | tf_op jit(solution)/shard_map/all_gather | solution.py:70
  16.1 5.8 %all_gather.66 = bf16[128,1024]{1,0:T(8,128)(2,1)S(1)} all-gather(bf16[64,1024]{1,0:T(8,128)(2,1)} %param.9), channel_id=1, replica_groups=mesh['row'=2,'col'=16] {'row'}, dimensions={0}, use_global_device_ids=true | all-gather | bytes 393216 | tf_op jit(solution)/shard_map/all_gather | solution.py:71
  22.5 31.8 %all-gather.20.cloned.1.call-done = bf16[1024,1024]{1,0:T(8,128)(2,1)} async-done(((bf16[64,1024]{1,0:T(8,128)(2,1)}), bf16[1024,1024]{1,0:T(8,128)(2,1)}) %all-gather.20.cloned.1.call-update) | async-done | bytes 2097168 | tf_op jit(solution)/shard_map/all_gather | solution.py:67
  54.3 2.9 fusion.37
  57.2 19.3 %all-gather.2 = f32[16384]{0:T(1024)S(1)} all-gather(f32[1024]{0:T(1024)S(1)} %get-tuple-element.112), channel_id=4, replica_groups=mesh['row'=2,'col'=16] {'col'}, dimensions={0}, use_global_device_ids=true | all-gather | bytes 69632 | tf_op jit(solution)/shard_map/all_gather | solution.py:10
  76.5 20.5 %all-gather.18.cloned.1.call-done = bf16[1024,1024]{1,0:T(8,128)(2,1)} async-done(((bf16[64,1024]{1,0:T(8,128)(2,1)}), bf16[1024,1024]{1,0:T(8,128)(2,1)}) %all-gather.18.cloned.1.call-update) | async-done | bytes 2097168 | tf_op jit(solution)/shard_map/all_gather | solution.py:66
  97.0 2.4 fusion.36
  99.4 19.4 %all-gather = f32[16384]{0:T(1024)S(1)} all-gather(f32[1024]{0:T(1024)S(1)} %get-tuple-element.110), channel_id=2, replica_groups=mesh['row'=2,'col'=16] {'col'}, dimensions={0}, use_global_device_ids=true | all-gather | bytes 69632 | tf_op jit(solution)/shard_map/all_gather | solution.py:10
  118.8 2.5 multiply_reduce_fusion
  121.4 17.6 %all-gather.4 = f32[16384]{0:T(1024)S(1)} all-gather(f32[1024]{0:T(1024)S(1)} %get-tuple-element.103), channel_id=6, replica_groups=mesh['row'=2,'col'=16] {'col'}, dimensions={0}, use_global_device_ids=true | all-gather | bytes 69632 | tf_op jit(solution)/shard_map/all_gather | solution.py:10
  139.6 18.9 %all-gather.3 = f32[16384]{0:T(1024)S(1)} all-gather(f32[1024]{0:T(1024)S(1)} %get-tuple-element.104), channel_id=5, replica_groups=mesh['row'=2,'col'=16] {'col'}, dimensions={0}, use_global_device_ids=true | all-gather | bytes 69632 | tf_op jit(solution)/shard_map/all_gather | solution.py:10
  159.1 17.6 %all-gather.1 = f32[16384]{0:T(1024)S(1)} all-gather(f32[1024]{0:T(1024)S(1)} %get-tuple-element.108), channel_id=3, replica_groups=mesh['row'=2,'col'=16] {'col'}, dimensions={0}, use_global_device_ids=true | all-gather | bytes 69632 | tf_op jit(solution)/shard_map/all_gather | solution.py:10
  177.4 4.2 %all-gather.13 = f32[2,1,128]{2,1,0:T(1,128)} all-gather(f32[1,1,128]{2,1,0:T(1,128)S(1)} %bitcast.195), channel_id=10, replica_groups=mesh['row'=2,'col'=16] {'row'}, dimensions={0}, use_global_device_ids=true | all-gather | bytes 1536 | tf_op jit(solution)/shard_map/all_gather | solution.py:10
  182.2 4.4 %all-gather.10 = f32[2,1,128]{2,1,0:T(1,128)S(1)} all-gather(f32[1,1,128]{2,1,0:T(1,128)} %bitcast.196), channel_id=7, replica_groups=mesh['row'=2,'col'=16] {'row'}, dimensions={0}, use_global_device_ids=true | all-gather | bytes 1536 | tf_op jit(solution)/shard_map/all_gather | solution.py:10
  186.6 4.4 %all-gather.14 = f32[2,1,128]{2,1,0:T(1,128)S(1)} all-gather(f32[1,1,128]{2,1,0:T(1,128)} %bitcast.199), channel_id=11, replica_groups=mesh['row'=2,'col'=16] {'row'}, dimensions={0}, use_global_device_ids=true | all-gather | bytes 1536 | tf_op jit(solution)/shard_map/all_gather | solution.py:10
  191.0 4.3 %all-gather.11 = f32[2,1,128]{2,1,0:T(1,128)S(1)} all-gather(f32[1,1,128]{2,1,0:T(1,128)} %bitcast.198), channel_id=8, replica_groups=mesh['row'=2,'col'=16] {'row'}, dimensions={0}, use_global_device_ids=true | all-gather | bytes 1536 | tf_op jit(solution)/shard_map/all_gather | solution.py:10
  195.9 0.8 reshape.44
  196.7 1.5 reshape.43
  198.2 1.5 reshape.41
  199.7 47.1 %while.2 = (s32[]{:T(128)}, f32[1024]{0:T(1024)S(1)}, f32[1024]{0:T(1024)S(1)}, f32[1024]{0:T(1024)S(1)}, f32[1024]{0:T(1024)S(1)}, /*index=5*/f32[1024]{0:T(102...) while((s32[]{:T(128)}, f32[1024]{0:T(1024)S(1)}, ...), condition=%wide.region_6.7_spmd, body=%wide.region_5.6_spmd.sunk | while | flops 17410 | bytes 123025 | solution.py:13
  199.7 0.8 constant_dynamic-slice_fusion.14
  202.8 0.8 constant_dynamic-slice_fusion.14
  209.1 0.8 constant_dynamic-slice_fusion.14
  212.3 0.8 constant_dynamic-slice_fusion.14
  215.4 0.8 constant_dynamic-slice_fusion.14
  221.7 0.8 constant_dynamic-slice_fusion.14
  224.8 0.8 constant_dynamic-slice_fusion.14
  247.5 2.7 convolution_multiply_fusion.1
  250.3 2.7 convolution_multiply_fusion
  253.6 4.2 %all-gather.12 = f32[2,1,128]{2,1,0:T(1,128)S(1)} all-gather(f32[1,1,128]{2,1,0:T(1,128)S(1)} %bitcast.197), channel_id=9, replica_groups=mesh['row'=2,'col'=16] {'row'}, dimensions={0}, use_global_device_ids=true | all-gather | bytes 1536 | tf_op jit(solution)/shard_map/all_gather | solution.py:10
  261.0 38.3 %psum.7 = f32[]{:T(128)} all-reduce(f32[]{:T(128)S(6)} %sub.142), channel_id=1, replica_groups=mesh['row'=2,'col'=16] {'row','col'}, use_global_device_ids=true, to_apply=%region_15.16 | all-reduce | flops 1 | bytes 8 | tf_op jit(solution)/shard_map/psum | solution.py:88
  300.0 40.8 %reduce-scatter.3.cloned.1.call-done = f32[64,1024]{1,0:T(8,128)} async-done(((f32[1024,1024]{1,0:T(8,128)}), f32[64,1024]{1,0:T(8,128)}) %reduce-scatter.3.cloned.1.call-update) | async-done | bytes 262160 | tf_op jit(solution)/shard_map/reduce_scatter | solution.py:97
  (154 shorter events, 49.1 us)
Async XLA Ops:
  7.2 47.2 %all-gather.20.cloned.1.call-start = ((), (), s32[]{:S(2)}) async-start(), calls=%async_computation.3 | async-start | bytes 2228224 | tf_op jit(solution)/shard_map/all_gather | solution.py:67
  7.9 89.1 %all-gather.18.cloned.1.call-start = ((), (), s32[]{:S(2)}) async-start(), calls=%async_computation.2 | async-start | bytes 2228224 | tf_op jit(solution)/shard_map/all_gather | solution.py:66
  8.6 291.4 %reduce-scatter.5.cloned.1.call-start = ((), (), s32[]{:S(2)}) async-start(), calls=%async_computation.5 | async-start | bytes 786432 | tf_op jit(solution)/shard_map/reduce_scatter | solution.py:104
  97.0 21.9 %copy-start.3 = (f32[128]{0:T(128)S(1)}, f32[128]{0:T(128)}, u32[]{:S(2)}) copy-start(f32[128]{0:T(128)} %get-tuple-element.111) | copy-start | bytes 1540
  99.4 78.0 %copy-start.4 = (f32[128]{0:T(128)}, f32[128]{0:T(128)S(1)}, u32[]{:S(2)}) copy-start(f32[128]{0:T(128)S(1)} %get-tuple-element.109) | copy-start | bytes 1540
  99.4 148.1 %copy-start = (bf16[1024,1024]{1,0:T(8,128)(2,1)S(1)}, bf16[1024,1024]{1,0:T(8,128)(2,1)}, u32[]{:S(2)}) copy-start(bf16[1024,1024]{1,0:T(8,128)(2,1)} %all-gather.18.cloned.1.call-done) | copy-start | bytes 6291460
  247.5 2.8 copy-start.1
  250.3 90.6 %reduce-scatter.3.cloned.1.call-start = ((), (), s32[]{:S(2)}) async-start(), calls=%async_computation.4 | async-start | bytes 4456448 | tf_op jit(solution)/shard_map/reduce_scatter | solution.py:97
  253.0 0.6 copy-start.5
  253.0 4.8 %copy-start.2 = (f32[2,1,128]{2,1,0:T(1,128)S(1)}, f32[2,1,128]{2,1,0:T(1,128)}, u32[]{:S(2)}) copy-start(f32[2,1,128]{2,1,0:T(1,128)} %all-gather.13) | copy-start | bytes 3076
Sparse Core Ops, SparseCore 0:
  10.1 44.1 all-gather.19
  56.5 40.4 all-gather.17
  250.4 13.1 reduce-scatter.4
  267.8 72.9 reduce-scatter.2
where the time goes:
time: 353 us; the launch traced here: 348 us
  blocking collectives  166 us (47%)
  waiting for transfers between devices  94.5 us (27%)
  local copies, waits for them, and re-layouts  53.7 us (15%)
  between operations  17.5 us (5%)
  matrix products  10.7 us (3%)
  other arithmetic  5.52 us (2%)
    all_gather x10, blocking collectives, joined(): pieces = jax.tree.map(lambda part: lax.all_gather(part, axis), value)  114 us
    dynamic_slice x75, local copies, waits for them, and re-layouts, joined(): lax.scan(lambda subtotal, slab: (join(subtotal, slab), None), head, tail)  46.1 us
    reduce_scatter x1, waiting for transfers between devices, body(): lax.psum_scatter(logit_scale * jnp.dot(picked, text_slab, preferred_eleme...  40.8 us
    psum x1, blocking collectives, body(): loss = lax.psum(partial_value, ('row', 'col')) / pair_count  38.3 us
    all_gather x1, waiting for transfers between devices, body(): lax.all_gather(image_teacher, 'col', axis=0, tiled=True)  31.8 us
    all_gather x1, waiting for transfers between devices, body(): lax.all_gather(image_student, 'col', axis=0, tiled=True)  20.5 us
    all_gather x1, blocking collectives, body(): lax.all_gather(text_student, 'row', axis=0, tiled=True)  7.42 us
  transfers between devices with their start and end apart: 4, of which 3 were waited for; matrix products, arithmetic and copies ran while one was open for 2% of the time, Pallas kernels for 0%

commit v1 on v0

v1 whole, which is shorter than its diff:
```python
import functools

import jax
import jax.numpy as jnp
from jax import lax
from jax.experimental import pallas as pl
from jax.experimental.pallas import tpu as pltpu
from jax.sharding import PartitionSpec as P

logit_scale = 100.0
MESH = pl.DeviceIdType.MESH
f32, bf16 = jnp.float32, jnp.bfloat16


def layout(mesh_shape):
    rows, cols = mesh_shape["row"], mesh_shape["col"]
    cores = 2 if cols % 2 == 0 else 1
    chips = cols // cores
    divisors = [d for d in range(1, chips + 1) if chips % d == 0]
    a = min(divisors, key=lambda d: d + rows * chips // d)
    q = max(d for d in range(1, a + 1) if a % d == 0 and d * d <= a)
    return dict(R=rows, C=cols, K=cores, A=a, H=chips // a, Q=q, P=a // q)


def contract_last(left, right):
    return lax.dot_general(left, right, (((1,), (1,)), ((), ())), preferred_element_type=f32)


def contract_first(left, right):
    return lax.dot_general(left, right, (((0,), (0,)), ((), ())), preferred_element_type=f32)


def merged(slots, count):
    def line(index, which):
        return slots[index, which : which + 1, :]

    student_high = functools.reduce(jnp.maximum, [line(i, 0) for i in range(count)])
    teacher_high = functools.reduce(jnp.maximum, [line(i, 2) for i in range(count)])
    student_total = teacher_total = divergence = 0.0
    for i in range(count):
        student_total += line(i, 1) * jnp.exp(line(i, 0) - student_high)
        factor = jnp.exp(line(i, 2) - teacher_high)
        teacher_total += line(i, 3) * factor
        divergence += line(i, 4) * factor
    student_lse = student_high + jnp.log(student_total)
    teacher_lse = teacher_high + jnp.log(teacher_total)
    kl = divergence / teacher_total - teacher_lse + student_lse
    return student_lse, teacher_lse, 0.5 * (student_lse + kl)


def position(index, step, count):
    total = jnp.zeros_like(index)
    for t in range(1, count):
        total += (index >= t * step).astype(jnp.int32)
    return total


def kernel(
    g, n_send, total,
    is_hbm, ts_hbm, it_hbm, tt_hbm,
    loss_ref, ig_ref, tg_ref,
    imgs, imgo, imgt, txts, txtt,
    s_ref, t_ref, rowtmp, rstat, cstat, la, lb, gbuf, grecv,
    pi, pib, pt, ptb, ri, rt,
    local_sem, send_sem, rimgs, rimgo, rimgt, rtxts, rtxtt, rrow, rcol, rla, rlb, rg, rri, rrt,
):
    R, K, A, H, Q, PP = g["R"], g["K"], g["A"], g["H"], g["Q"], g["P"]
    n = is_hbm.shape[0]
    r = lax.axis_index("row")
    c = lax.axis_index("col")
    k, chip = lax.rem(c, K), lax.div(c, K)
    lo, hi = lax.rem(chip, A), lax.div(chip, A)
    q, p = lax.rem(lo, Q), lax.div(lo, Q)
    HR, T = H * R, K * H * R

    def dev(r_, hi_, lo_, k_):
        return (r_, (hi_ * A + lo_) * K + k_)

    def up(value, step, count):
        return lax.rem(value + step, count)

    def down(value, step, count):
        return lax.rem(value + count - step, count)

    def block(ref, index):
        return ref.at[pl.ds(pl.multiple_of(index * n, n), n), :]

    a_peers = [dev(r, hi, up(lo, d, A), k) for d in range(1, A)]
    b_steps = [(dk, dh, dr) for dk in range(K) for dh in range(H) for dr in range(R)]
    b_peers = [dev(up(r, dr, R), up(hi, dh, H), lo, up(k, dk, K)) for dk, dh, dr in b_steps[1:]]
    partner = dev(r, hi, lo, up(k, 1, K))

    pending = []

    def send(src, dst, recv, target):
        copy = pltpu.make_async_remote_copy(
            src_ref=src, dst_ref=dst, send_sem=send_sem.at[len(pending)], recv_sem=recv,
            device_id=target, device_id_type=MESH,
        )
        copy.start()
        pending.append(copy)

    def arrived(ref, recv):
        pltpu.make_async_remote_copy(
            src_ref=ref, dst_ref=ref, send_sem=send_sem.at[0], recv_sem=recv,
            device_id=partner, device_id_type=MESH,
        ).wait_recv()

    own_text = (k * H + hi) * R + r
    loads = []
    for i, (src, dst) in enumerate((
        (is_hbm, block(imgs, lo)), (ts_hbm, block(txts, own_text)),
        (it_hbm, block(imgt, lo)), (tt_hbm, block(txtt, own_text)),
    )):
        copy = pltpu.make_async_copy(src, dst, local_sem.at[i])
        copy.start()
        loads.append(copy)
    barrier = pltpu.get_barrier_semaphore()
    for target in a_peers + b_peers:
        pl.semaphore_signal(barrier, inc=1, device_id=target, device_id_type=MESH)
    pl.semaphore_wait(barrier, len(a_peers) + len(b_peers))

    def image_slot(dp, dq):
        return down(p, dp, PP) * Q + down(q, dq, Q)

    def text_slot(dk, dh, dr):
        return (down(k, dk, K) * H + down(hi, dh, H)) * R + down(r, dr, R)

    def image_own(ref, sems):
        for dp in range(1, PP):
            send(block(ref, lo), block(ref, lo), sems.at[dp * Q], dev(r, hi, up(p, dp, PP) * Q + q, k))

    def image_spread(ref, sems, dp):
        slot = image_slot(dp, 0)
        for dq in range(1, Q):
            send(block(ref, slot), block(ref, slot), sems.at[dp * Q + dq],
                 dev(r, hi, p * Q + up(q, dq, Q), k))

    def text_own(ref, sems):
        for dh in range(1, H):
            send(block(ref, own_text), block(ref, own_text), sems.at[dh * R],
                 dev(r, up(hi, dh, H), lo, k))

    def text_spread(ref, sems, dh):
        slot = text_slot(0, dh, 0)
        for dr in range(1, R):
            send(block(ref, slot), block(ref, slot), sems.at[dh * R + dr],
                 dev(up(r, dr, R), hi, lo, k))

    def text_across(ref, sems, dh, dr):
        slot = text_slot(0, dh, dr)
        for dk in range(1, K):
            send(block(ref, slot), block(ref, slot), sems.at[(dk * H + dh) * R + dr],
                 dev(r, hi, lo, up(k, dk, K)))

    pairs = ((imgs, rimgs, txts, rtxts), (imgt, rimgt, txtt, rtxtt))
    for i, (img, rimg, txt, rtxt) in enumerate(pairs):
        loads[2 * i].wait()
        image_own(img, rimg)
        loads[2 * i + 1].wait()
        text_own(txt, rtxt)
        image_spread(img, rimg, 0)
        text_spread(txt, rtxt, 0)
        text_across(txt, rtxt, 0, 0)

    def forward(img, rimg, txt, rtxt):
        for dp in range(1, PP):
            arrived(block(img, image_slot(dp, 0)), rimg.at[dp * Q])
            image_spread(img, rimg, dp)
        for dh in range(1, H):
            arrived(block(txt, text_slot(0, dh, 0)), rtxt.at[dh * R])
            text_spread(txt, rtxt, dh)
            text_across(txt, rtxt, dh, 0)

    def collect(img, rimg, txt, rtxt):
        for dh in range(H):
            for dr in range(1, R):
                arrived(block(txt, text_slot(0, dh, dr)), rtxt.at[dh * R + dr])
                text_across(txt, rtxt, dh, dr)
        for dp in range(PP):
            for dq in range(1, Q):
                arrived(block(img, image_slot(dp, dq)), rimg.at[dp * Q + dq])
        for dk, dh, dr in b_steps:
            if dk:
                arrived(block(txt, text_slot(dk, dh, dr)), rtxt.at[(dk * H + dh) * R + dr])

    for pair in pairs:
        forward(*pair)
    collect(*pairs[0])
    s_ref[...] = logit_scale * contract_last(imgs[...], txts[...])
    collect(*pairs[1])
    if K > 1:
        send(imgs, imgo, rimgo, partner)
    t_ref[...] = logit_scale * contract_last(imgt[...], txtt[...])

    rows, width = s_ref.shape
    col_s = jnp.max(s_ref[...], axis=0, keepdims=True)
    col_t = jnp.max(t_ref[...], axis=0, keepdims=True)
    lane = lax.broadcasted_iota(jnp.int32, (n, 128), 1)
    col_id = lax.broadcasted_iota(jnp.int32, (1, width), 1)
    col_slot = position(col_id, n, T)
    slot_k, slot_h = position(col_slot, HR, K), position(col_slot, R, K * H)
    slot_r = col_slot - slot_h * R
    slot_h = slot_h - slot_k * H
    col_id = (((slot_h * A + lo) * K + slot_k) * R + slot_r) * n + col_id - col_slot * n
    row_id = lax.broadcasted_iota(jnp.int32, (n, 1), 0)
    sums = [0.0] * 3
    diagonal = 0.0

    def eye(b):
        base = (r * g["C"] + (hi * A + b) * K + k) * n
        return row_id + base == col_id

    for b in range(A):
        at = slice(b * n, (b + 1) * n)
        s, t = s_ref[at, :], t_ref[at, :]
        gap = t - s
        row_s = jnp.max(s, axis=1, keepdims=True)
        row_t = jnp.max(t, axis=1, keepdims=True)
        row_weight = jnp.exp(t - row_t)
        stats = (
            row_s,
            jnp.sum(jnp.exp(s - row_s), axis=1, keepdims=True),
            row_t,
            jnp.sum(row_weight, axis=1, keepdims=True),
            jnp.sum(row_weight * gap, axis=1, keepdims=True),
        )
        packed = jnp.zeros((n, 128), f32)
        for i, value in enumerate(stats):
            packed = jnp.where(lane == i, value, packed)
        rowtmp[at, :] = packed
        col_weight = jnp.exp(t - col_t)
        parts = (jnp.exp(s - col_s), col_weight, col_weight * gap)
        sums = [old + jnp.sum(new, axis=0, keepdims=True) for old, new in zip(sums, parts)]
        diagonal += jnp.sum(jnp.where(eye(b), s, 0.0), axis=0, keepdims=True)
    line = lax.broadcasted_iota(jnp.int32, (8, width), 0)
    packed = jnp.zeros((8, width), f32)
    for i, value in enumerate((col_s, sums[0], col_t, sums[1], sums[2])):
        packed = jnp.where(line == i, value, packed)
    cstat[0] = packed
    for e, target in enumerate(b_peers, 1):
        send(cstat.at[0], cstat.at[e], rcol.at[e], target)
    rstat[0] = jnp.transpose(rowtmp[...])[:8, :]
    for d, target in enumerate(a_peers, 1):
        send(rstat.at[0], rstat.at[d], rrow.at[d], target)
    for d in range(1, A):
        arrived(rstat.at[d], rrow.at[d])
    row_student, row_teacher, row_terms = merged(rstat, A)
    line = lax.broadcasted_iota(jnp.int32, (128, rows), 0)
    rowtmp[...] = jnp.transpose(jnp.where(line == 0, row_student, row_teacher))
    for e in range(1, T):
        arrived(cstat.at[e], rcol.at[e])
    col_student, col_teacher, col_terms = merged(cstat, T)

    at_row = lax.broadcasted_iota(jnp.int32, (1, rows), 1) - lo * n
    at_col = lax.broadcasted_iota(jnp.int32, (1, width), 1) - own_text * n
    share = (
        jnp.sum(jnp.where((at_row >= 0) & (at_row < n), row_terms, 0.0), axis=1, keepdims=True)
        + jnp.sum(
            jnp.where((at_col >= 0) & (at_col < n), col_terms, 0.0) - diagonal,
            axis=1, keepdims=True,
        )
    )
    la[0] = jnp.broadcast_to(share, (8, 128))
    for d, target in enumerate(a_peers, 1):
        send(la.at[0], la.at[d], rla.at[d], target)

    half = width // K
    for b in range(A):
        at = slice(b * n, (b + 1) * n)
        s, t = s_ref[at, :], t_ref[at, :]
        row_s, row_t = rowtmp[at, 0:1], rowtmp[at, 1:2]
        grad = (
            jnp.exp(s - row_s) + jnp.exp(s - col_student)
            - 0.5 * (jnp.exp(t - row_t) + jnp.exp(t - col_teacher))
            - jnp.where(eye(b), 1.0, 0.0)
        ).astype(bf16)
        for j in range(K):
            gbuf[j, at, :] = grad[:, j * half : (j + 1) * half]
    if K > 1:
        send(gbuf.at[up(k, 1, K)], grecv, rg, partner)

    partial = 0.0
    for j in range(K):
        partial += jnp.dot(gbuf[j], txts[j * half : (j + 1) * half, :], preferred_element_type=f32)
    pi[...] = partial
    pib[...] = partial.astype(bf16)
    for d, target in enumerate(a_peers, 1):
        send(block(pib, up(lo, d, A)), ri.at[d - 1], rri.at[d], target)

    for d in range(1, A):
        arrived(la.at[d], rla.at[d])
    lb[0] = functools.reduce(jnp.add, [la[d] for d in range(A)])
    for e, target in enumerate(b_peers, 1):
        send(lb.at[0], lb.at[e], rlb.at[e], target)

    if K > 1:
        arrived(imgo, rimgo)
        arrived(grecv, rg)
    partial = contract_first(gbuf[k], imgs[...])
    if K > 1:
        partial += contract_first(grecv[...], imgo[...])
    pt[...] = partial
    ptb[...] = partial.astype(bf16)
    for dh in range(H):
        for dr in range(R):
            if dh or dr:
                send(block(ptb, up(hi, dh, H) * R + up(r, dr, R)), rt.at[dh * R + dr - 1],
                     rrt.at[dh * R + dr], dev(up(r, dr, R), up(hi, dh, H), lo, k))

    for e in range(1, T):
        arrived(lb.at[e], rlb.at[e])
    loss_ref[...] = functools.reduce(jnp.add, [lb[e] for e in range(T)]) / total
    for d in range(1, A):
        arrived(ri.at[d - 1], rri.at[d])
    value = block(pi, lo)[...]
    for d in range(1, A):
        value += ri[d - 1].astype(f32)
    ig_ref[...] = logit_scale * value
    for e in range(1, HR):
        arrived(rt.at[e - 1], rrt.at[e])
    value = block(pt, hi * R + r)[...]
    for e in range(1, HR):
        value += rt[e - 1].astype(f32)
    tg_ref[...] = logit_scale * value
    for copy in pending:
        copy.wait_send()
    assert len(pending) == n_send, len(pending)


def solution(mesh):
    g = layout(mesh.shape)
    R, K, A, H, Q, PP = g["R"], g["K"], g["A"], g["H"], g["Q"], g["P"]
    HR, T = H * R, K * H * R
    gather = 2 * (A - 1) + 2 * (HR - 1) + 2 * HR * (K - 1) + (K - 1)
    n_send = gather + 2 * (A - 1) + 2 * (T - 1) + (K - 1) + (A - 1) + (HR - 1)

    def body(image_student, text_student, image_teacher, text_teacher):
        n, width = image_student.shape
        rows, cols = A * n, T * n
        total = n * R * g["C"]
        vmem, dma = pltpu.VMEM, pltpu.SemaphoreType.DMA
        block_out = jax.ShapeDtypeStruct((n, width), f32)
        loss, image_grad, text_grad = pl.pallas_call(
            functools.partial(kernel, g, n_send, total),
            out_shape=(jax.ShapeDtypeStruct((8, 128), f32), block_out, block_out),
            in_specs=[pl.BlockSpec(memory_space=pl.ANY)] * 4,
            out_specs=[pl.BlockSpec(memory_space=pltpu.VMEM)] * 3,
            scratch_shapes=[
                vmem((rows, width), bf16), vmem((rows, width), bf16), vmem((rows, width), bf16),
                vmem((cols, width), bf16), vmem((cols, width), bf16),
                vmem((rows, cols), f32), vmem((rows, cols), f32),
                vmem((rows, 128), f32), vmem((A, 8, rows), f32), vmem((T, 8, cols), f32),
                vmem((A, 8, 128), f32), vmem((T, 8, 128), f32),
                vmem((K, rows, cols // K), bf16), vmem((rows, cols // K), bf16),
                vmem((rows, width), f32), vmem((rows, width), bf16),
                vmem((cols // K, width), f32), vmem((cols // K, width), bf16),
                vmem((max(A - 1, 1), n, width), bf16), vmem((max(HR - 1, 1), n, width), bf16),
                dma((4,)), dma((n_send,)),
                dma((A,)), dma(()), dma((A,)), dma((T,)), dma((T,)),
                dma((A,)), dma((T,)), dma((A,)), dma((T,)), dma(()), dma((A,)), dma((HR,)),
            ],
            compiler_params=pltpu.CompilerParams(
                collective_id=0, has_side_effects=True, vmem_limit_bytes=56 * 1024 * 1024
            ),
        )(image_student, text_student, image_teacher, text_teacher)
        return loss[0, 0], image_grad, text_grad

    return jax.shard_map(
        body,
        mesh=mesh,
        in_specs=(
            P(("row", "col"), None),
            P(("col", "row"), None),
            P(("row", "col"), None),
            P(("col", "row"), None),
        ),
        out_specs=(P(), P(("row", "col"), None), P(("col", "row"), None)),
        check_vma=False,
    )
```

time: 353 us -> 53 us (0.15); the launches traced: 348 us -> 52.9 us
  blocking collectives: 166 us -> 0 us
  waiting for transfers between devices: 94.5 us -> 0 us
  local copies, waits for them, and re-layouts: 53.7 us -> 3.61 us
  Pallas kernels: 0 us -> 48.6 us
  between operations: 17.5 us -> 0.64 us
  matrix products: 10.7 us -> 0 us
  other arithmetic: 5.52 us -> 0 us
    all_gather x12 -> x0, blocking collectives: 128 us -> none  [the longest x10 114 us: joined(): pieces = jax.tree.map(lambda part: lax.all_gather(part, axis), value)]
    all_gather x2 -> x0, waiting for transfers between devices: 52.3 us -> none  [the longest x1 31.8 us: body(): lax.all_gather(image_teacher, 'col', axis=0, tiled=True)]
    pallas_call x0 -> x1, Pallas kernels: none -> 48.6 us  [body(): pl.pallas_call(functools.partial(kernel, g, n_send, total), out_shape=(ja...]
    dynamic_slice x75 -> x0, local copies, waits for them, and re-layouts: 46.1 us -> none  [joined(): lax.scan(lambda subtotal, slab: (join(subtotal, slab), None), head, tail)]
    reduce_scatter x2 -> x0, waiting for transfers between devices: 40.8 us -> none  [the longest x1 40.8 us: body(): lax.psum_scatter(logit_scale * jnp.dot(picked, text_slab, preferred_eleme...]
    psum x1 -> x0, blocking collectives: 38.3 us -> none  [body(): loss = lax.psum(partial_value, ('row', 'col')) / pair_count]
    dot_general x4 -> x0, matrix products: 10.7 us -> none  [the longest x2 5.28 us: tile_logits(): lax.dot_general(left, right, (((1,), (1,)), ((), ())), preferred_element_...]
    slice x15 -> x1, local copies, waits for them, and re-layouts: 6.92 us -> 1.19 us  [body(): return (loss[0, 0], image_grad, text_grad)]
  transfers between devices with their start and end apart: 4 -> 0, of which waited for: 3 -> 0; matrix products, arithmetic and copies ran while one was open for 2% -> 0% of each run, Pallas kernels for 0% -> 0%
where the time goes in v1:
time: 53 us; the launch traced here: 52.9 us
  Pallas kernels  48.6 us (92%)
  local copies, waits for them, and re-layouts  3.61 us (7%)
  between operations  0.64 us (1%)
    pallas_call x1, Pallas kernels, body(): pl.pallas_call(functools.partial(kernel, g, n_send, total), out_shape=(ja...  48.6 us
    unnamed x4, local copies, waits for them, and re-layouts  2.42 us
    slice x1, local copies, waits for them, and re-layouts, body(): return (loss[0, 0], image_grad, text_grad)  1.19 us

profile of v1, /device:TPU:0, one launch (start us, length us, event | category | flops | bytes accessed | tf_op | source)
XLA Modules:
  0.0 52.9 jit_solution(14927984663083863462)
XLA Ops:
  0.6 48.6 %shard_map.67 = (f32[8,128]{1,0:T(8,128)}, f32[64,1024]{1,0:T(8,128)}, f32[64,1024]{1,0:T(8,128)}) custom-call(bf16[64,1024]{1,0:T(8,128)(2,1)} %is_hbm.1, bf16[64,1024]{1,0:T(8,128)(2,1)} %ts_hbm.1, bf16[64,1024]{1,0:T(8,128)(2,1)} %it_hbm.1, bf16[64,1024]{1,0:T(8,128)(2,1)} %tt_hbm.1), custom_call_target="tpu_custom_call" | custom-call | tf_op jit(solution)/shard_map/pallas_call | solution.py:344
  49.2 1.2 %slice.3 = f32[1,1]{1,0:T(1,128)} slice(f32[8,128]{1,0:T(8,128)} %get-tuple-element.6), slice={[0:1], [0:1]} | slice | bytes 8 | tf_op jit(solution)/shard_map/slice | solution.py:367
  50.4 0.0 copy-start
  50.4 1.7 %copy.9 = f32[64,1024]{1,0:T(8,128)} copy(f32[64,1024]{1,0:T(8,128)} %get-tuple-element.13) | data formatting | bytes 524288
  52.1 0.0 copy-done
  52.1 0.7 %copy.10 = f32[64,1024]{1,0:T(8,128)} copy(f32[64,1024]{1,0:T(8,128)S(1)} %copy-done) | data formatting | bytes 524288
Async XLA Ops:
  50.4 1.7 %copy-start = (f32[64,1024]{1,0:T(8,128)S(1)}, f32[64,1024]{1,0:T(8,128)}, u32[]{:S(2)}) copy-start(f32[64,1024]{1,0:T(8,128)} %get-tuple-element.14) | copy-start | bytes 786436

commit v2 on v1

--- a/solution.py
+++ b/solution.py
@@ -61,11 +61,13 @@
     loss_ref, ig_ref, tg_ref,
     imgs, imgo, imgt, txts, txtt,
     s_ref, t_ref, rowtmp, rstat, cstat, la, lb, gbuf, grecv,
-    pi, pib, pt, ptb, ri, rt,
-    local_sem, send_sem, rimgs, rimgo, rimgt, rtxts, rtxtt, rrow, rcol, rla, rlb, rg, rri, rrt,
+    pi, inarrow, inear, idirect, ijoint, ifar, pt, tnarrow, tnear, tdirect, tjoint, tfar,
+    local_sem, send_sem, rimgs, rimgo, rimgt, rtxts, rtxtt, rrow, rcol, rla, rlb, rg,
+    rinear, ridirect, rifar, rtnear, rtdirect, rtfar,
 ):
     R, K, A, H, Q, PP = g["R"], g["K"], g["A"], g["H"], g["Q"], g["P"]
-    n = is_hbm.shape[0]
+    n, S = is_hbm.shape[0], g["S"]
+    m = n // S
     r = lax.axis_index("row")
     c = lax.axis_index("col")
     k, chip = lax.rem(c, K), lax.div(c, K)
@@ -84,6 +86,9 @@
 
     def block(ref, index):
         return ref.at[pl.ds(pl.multiple_of(index * n, n), n), :]
+
+    def piece(ref, index, j):
+        return ref.at[pl.ds(pl.multiple_of(index * n + j * m, m), m), :]
 
     a_peers = [dev(r, hi, up(lo, d, A), k) for d in range(1, A)]
     b_steps = [(dk, dh, dr) for dk in range(K) for dh in range(H) for dr in range(R)]
@@ -126,63 +131,72 @@
     def text_slot(dk, dh, dr):
         return (down(k, dk, K) * H + down(hi, dh, H)) * R + down(r, dr, R)
 
-    def image_own(ref, sems):
+    def text_at(dk, dh, dr):
+        return (dk * H + dh) * R + dr
+
+    def image_own(ref, sems, j):
         for dp in range(1, PP):
-            send(block(ref, lo), block(ref, lo), sems.at[dp * Q], dev(r, hi, up(p, dp, PP) * Q + q, k))
-
-    def image_spread(ref, sems, dp):
+            send(piece(ref, lo, j), piece(ref, lo, j), sems.at[dp * Q, j],
+                 dev(r, hi, up(p, dp, PP) * Q + q, k))
+
+    def image_spread(ref, sems, dp, j):
         slot = image_slot(dp, 0)
         for dq in range(1, Q):
-            send(block(ref, slot), block(ref, slot), sems.at[dp * Q + dq],
+            send(piece(ref, slot, j), piece(ref, slot, j), sems.at[dp * Q + dq, j],
                  dev(r, hi, p * Q + up(q, dq, Q), k))
 
-    def text_own(ref, sems):
+    def text_own(ref, sems, j):
         for dh in range(1, H):
-            send(block(ref, own_text), block(ref, own_text), sems.at[dh * R],
+            send(piece(ref, own_text, j), piece(ref, own_text, j), sems.at[text_at(0, dh, 0), j],
                  dev(r, up(hi, dh, H), lo, k))
 
-    def text_spread(ref, sems, dh):
+    def text_spread(ref, sems, dh, j):
         slot = text_slot(0, dh, 0)
         for dr in range(1, R):
-            send(block(ref, slot), block(ref, slot), sems.at[dh * R + dr],
+            send(piece(ref, slot, j), piece(ref, slot, j), sems.at[text_at(0, dh, dr), j],
                  dev(up(r, dr, R), hi, lo, k))
 
-    def text_across(ref, sems, dh, dr):
+    def text_across(ref, sems, dh, dr, j):
         slot = text_slot(0, dh, dr)
         for dk in range(1, K):
-            send(block(ref, slot), block(ref, slot), sems.at[(dk * H + dh) * R + dr],
+            send(piece(ref, slot, j), piece(ref, slot, j), sems.at[text_at(dk, dh, dr), j],
                  dev(r, hi, lo, up(k, dk, K)))
 
     pairs = ((imgs, rimgs, txts, rtxts), (imgt, rimgt, txtt, rtxtt))
     for i, (img, rimg, txt, rtxt) in enumerate(pairs):
         loads[2 * i].wait()
-        image_own(img, rimg)
         loads[2 * i + 1].wait()
-        text_own(txt, rtxt)
-        image_spread(img, rimg, 0)
-        text_spread(txt, rtxt, 0)
-        text_across(txt, rtxt, 0, 0)
+        for j in range(S):
+            image_own(img, rimg, j)
+            text_own(txt, rtxt, j)
+        for j in range(S):
+            image_spread(img, rimg, 0, j)
+            text_spread(txt, rtxt, 0, j)
+            text_across(txt, rtxt, 0, 0, j)
 
     def forward(img, rimg, txt, rtxt):
-        for dp in range(1, PP):
-            arrived(block(img, image_slot(dp, 0)), rimg.at[dp * Q])
-            image_spread(img, rimg, dp)
-        for dh in range(1, H):
-            arrived(block(txt, text_slot(0, dh, 0)), rtxt.at[dh * R])
-            text_spread(txt, rtxt, dh)
-            text_across(txt, rtxt, dh, 0)
+        for j in range(S):
+            for dp in range(1, PP):
+                arrived(piece(img, image_slot(dp, 0), j), rimg.at[dp * Q, j])
+                image_spread(img, rimg, dp, j)
+            for dh in range(1, H):
+                arrived(piece(txt, text_slot(0, dh, 0), j), rtxt.at[text_at(0, dh, 0), j])
+                text_spread(txt, rtxt, dh, j)
+                text_across(txt, rtxt, dh, 0, j)
 
     def collect(img, rimg, txt, rtxt):
         for dh in range(H):
-            for dr in range(1, R):
-                arrived(block(txt, text_slot(0, dh, dr)), rtxt.at[dh * R + dr])
-                text_across(txt, rtxt, dh, dr)
-        for dp in range(PP):
-            for dq in range(1, Q):
-                arrived(block(img, image_slot(dp, dq)), rimg.at[dp * Q + dq])
-        for dk, dh, dr in b_steps:
-            if dk:
-                arrived(block(txt, text_slot(dk, dh, dr)), rtxt.at[(dk * H + dh) * R + dr])
+            for j in range(S):
+                for dr in range(1, R):
+                    arrived(piece(txt, text_slot(0, dh, dr), j), rtxt.at[text_at(0, dh, dr), j])
+                    text_across(txt, rtxt, dh, dr, j)
+        for j in range(S):
+            for dp in range(PP):
+                for dq in range(1, Q):
+                    arrived(piece(img, image_slot(dp, dq), j), rimg.at[dp * Q + dq, j])
+            for dk, dh, dr in b_steps:
+                if dk:
+                    arrived(piece(txt, text_slot(dk, dh, dr), j), rtxt.at[text_at(dk, dh, dr), j])
 
     for pair in pairs:
         forward(*pair)
@@ -284,15 +298,49 @@
     for j in range(K):
         partial += jnp.dot(gbuf[j], txts[j * half : (j + 1) * half, :], preferred_element_type=f32)
     pi[...] = partial
-    pib[...] = partial.astype(bf16)
-    for d, target in enumerate(a_peers, 1):
-        send(block(pib, up(lo, d, A)), ri.at[d - 1], rri.at[d], target)
-
-    for d in range(1, A):
-        arrived(la.at[d], rla.at[d])
-    lb[0] = functools.reduce(jnp.add, [la[d] for d in range(A)])
-    for e, target in enumerate(b_peers, 1):
-        send(lb.at[0], lb.at[e], rlb.at[e], target)
+
+    def first_hops(part, out_index, in_index, outer, inner, narrow, near, nears, direct, directs, target):
+        for j in range(S):
+            for do in range(1, outer):
+                for di in range(1, inner):
+                    e = (do - 1) * (inner - 1) + di - 1
+                    to = up(in_index, di, inner)
+                    send(piece(part, up(out_index, do, outer) * inner + to, j), piece(near, e, j),
+                         nears.at[e, j], target(out_index, to))
+        for di in range(1, inner):
+            to = up(in_index, di, inner)
+            block(narrow, di - 1)[...] = block(part, out_index * inner + to)[...].astype(bf16)
+            send(block(narrow, di - 1), block(direct, di - 1), directs.at[di - 1], target(out_index, to))
+
+    def second_hops(part, out_index, in_index, outer, inner, near, nears, joint, far, fars, target, j):
+        for do in range(1, outer):
+            to = up(out_index, do, outer)
+            value = piece(part, to * inner + in_index, j)[...]
+            for di in range(1, inner):
+                e = (do - 1) * (inner - 1) + di - 1
+                arrived(piece(near, e, j), nears.at[e, j])
+                value += piece(near, e, j)[...]
+            piece(joint, do - 1, j)[...] = value.astype(bf16)
+            send(piece(joint, do - 1, j), piece(far, do - 1, j), fars.at[do - 1, j], target(to, in_index))
+
+    def last_sum(part, out_index, in_index, outer, inner, direct, directs, far, fars):
+        value = block(part, out_index * inner + in_index)[...]
+        for di in range(1, inner):
+            arrived(block(direct, di - 1), directs.at[di - 1])
+            value += block(direct, di - 1)[...].astype(f32)
+        for do in range(1, outer):
+            for j in range(S):
+                arrived(piece(far, do - 1, j), fars.at[do - 1, j])
+            value += block(far, do - 1)[...].astype(f32)
+        return logit_scale * value
+
+    def image_target(p_, q_):
+        return dev(r, hi, p_ * Q + q_, k)
+
+    def text_target(h_, r_):
+        return dev(r_, h_, lo, k)
+
+    first_hops(pi, p, q, PP, Q, inarrow, inear, rinear, idirect, ridirect, image_target)
 
     if K > 1:
         arrived(imgo, rimgo)
@@ -301,28 +349,22 @@
     if K > 1:
         partial += contract_first(grecv[...], imgo[...])
     pt[...] = partial
-    ptb[...] = partial.astype(bf16)
-    for dh in range(H):
-        for dr in range(R):
-            if dh or dr:
-                send(block(ptb, up(hi, dh, H) * R + up(r, dr, R)), rt.at[dh * R + dr - 1],
-                     rrt.at[dh * R + dr], dev(up(r, dr, R), up(hi, dh, H), lo, k))
+    first_hops(pt, hi, r, H, R, tnarrow, tnear, rtnear, tdirect, rtdirect, text_target)
+    for j in range(S):
+        second_hops(pi, p, q, PP, Q, inear, rinear, ijoint, ifar, rifar, image_target, j)
+        second_hops(pt, hi, r, H, R, tnear, rtnear, tjoint, tfar, rtfar, text_target, j)
+        if j == 0:
+            for d in range(1, A):
+                arrived(la.at[d], rla.at[d])
+            lb[0] = functools.reduce(jnp.add, [la[d] for d in range(A)])
+            for e, target in enumerate(b_peers, 1):
+                send(lb.at[0], lb.at[e], rlb.at[e], target)
 
     for e in range(1, T):
         arrived(lb.at[e], rlb.at[e])
     loss_ref[...] = functools.reduce(jnp.add, [lb[e] for e in range(T)]) / total
-    for d in range(1, A):
-        arrived(ri.at[d - 1], rri.at[d])
-    value = block(pi, lo)[...]
-    for d in range(1, A):
-        value += ri[d - 1].astype(f32)
-    ig_ref[...] = logit_scale * value
-    for e in range(1, HR):
-        arrived(rt.at[e - 1], rrt.at[e])
-    value = block(pt, hi * R + r)[...]
-    for e in range(1, HR):
-        value += rt[e - 1].astype(f32)
-    tg_ref[...] = logit_scale * value
+    ig_ref[...] = last_sum(pi, p, q, PP, Q, idirect, ridirect, ifar, rifar)
+    tg_ref[...] = last_sum(pt, hi, r, H, R, tdirect, rtdirect, tfar, rtfar)
     for copy in pending:
         copy.wait_send()
     assert len(pending) == n_send, len(pending)
@@ -332,14 +374,28 @@
     g = layout(mesh.shape)
     R, K, A, H, Q, PP = g["R"], g["K"], g["A"], g["H"], g["Q"], g["P"]
     HR, T = H * R, K * H * R
-    gather = 2 * (A - 1) + 2 * (HR - 1) + 2 * HR * (K - 1) + (K - 1)
-    n_send = gather + 2 * (A - 1) + 2 * (T - 1) + (K - 1) + (A - 1) + (HR - 1)
+    near = ((PP - 1) * (Q - 1), (H - 1) * (R - 1))
 
     def body(image_student, text_student, image_teacher, text_teacher):
         n, width = image_student.shape
         rows, cols = A * n, T * n
         total = n * R * g["C"]
+        S = g["S"] = 4 if n % 64 == 0 else 1
+        gather = S * (2 * (A - 1) + 2 * (HR - 1) + 2 * HR * (K - 1)) + (K - 1)
+        n_send = gather + 2 * (A - 1) + 2 * (T - 1) + (K - 1)
+        n_send += S * (sum(near) + PP - 1 + H - 1) + Q - 1 + R - 1
         vmem, dma = pltpu.VMEM, pltpu.SemaphoreType.DMA
+
+        def sums(size, near, direct, far):
+            near, direct, far = max(near, 1) * n, max(direct, 1) * n, max(far, 1) * n
+            return (
+                vmem((size, width), f32), vmem((direct, width), bf16), vmem((near, width), f32),
+                vmem((direct, width), bf16), vmem((far, width), bf16), vmem((far, width), bf16),
+            )
+
+        def arrivals(near, direct, far):
+            return dma((max(near, 1), S)), dma((max(direct, 1),)), dma((max(far, 1), S))
+
         block_out = jax.ShapeDtypeStruct((n, width), f32)
         loss, image_grad, text_grad = pl.pallas_call(
             functools.partial(kernel, g, n_send, total),
@@ -353,12 +409,11 @@
                 vmem((rows, 128), f32), vmem((A, 8, rows), f32), vmem((T, 8, cols), f32),
                 vmem((A, 8, 128), f32), vmem((T, 8, 128), f32),
                 vmem((K, rows, cols // K), bf16), vmem((rows, cols // K), bf16),
-                vmem((rows, width), f32), vmem((rows, width), bf16),
-                vmem((cols // K, width), f32), vmem((cols // K, width), bf16),
-                vmem((max(A - 1, 1), n, width), bf16), vmem((max(HR - 1, 1), n, width), bf16),
+                *sums(rows, near[0], Q - 1, PP - 1), *sums(cols // K, near[1], R - 1, H - 1),
                 dma((4,)), dma((n_send,)),
-                dma((A,)), dma(()), dma((A,)), dma((T,)), dma((T,)),
-                dma((A,)), dma((T,)), dma((A,)), dma((T,)), dma(()), dma((A,)), dma((HR,)),
+                dma((A, S)), dma(()), dma((A, S)), dma((T, S)), dma((T, S)),
+                dma((A,)), dma((T,)), dma((A,)), dma((T,)), dma(()),
+                *arrivals(near[0], Q - 1, PP - 1), *arrivals(near[1], R - 1, H - 1),
             ],
             compiler_params=pltpu.CompilerParams(
                 collective_id=0, has_side_effects=True, vmem_limit_bytes=56 * 1024 * 1024

time: 53 us -> 50.3 us (0.949)
  Pallas kernels: 48.6 us -> 45.9 us
    pallas_call x1, Pallas kernels: 48.6 us -> 45.9 us  [body(): pl.pallas_call(functools.partial(kernel, g, n_send, total), out_shape=(ja...]
where the time goes in v2:
time: 50.3 us; the launch traced here: 50.1 us
  Pallas kernels  45.9 us (91%)
  local copies, waits for them, and re-layouts  3.61 us (7%)
  between operations  0.64 us (1%)
    pallas_call x1, Pallas kernels, body(): pl.pallas_call(functools.partial(kernel, g, n_send, total), out_shape=(ja...  45.9 us
    unnamed x4, local copies, waits for them, and re-layouts  2.42 us
    slice x1, local copies, waits for them, and re-layouts, body(): return (loss[0, 0], image_grad, text_grad)  1.19 us

profile of v2, /device:TPU:0, one launch (start us, length us, event | category | flops | bytes accessed | tf_op | source)
XLA Modules:
  0.0 50.1 jit_solution(11588603240790148295)
XLA Ops:
  0.6 45.9 %shard_map.67 = (f32[8,128]{1,0:T(8,128)}, f32[64,1024]{1,0:T(8,128)}, f32[64,1024]{1,0:T(8,128)}) custom-call(bf16[64,1024]{1,0:T(8,128)(2,1)} %is_hbm.1, bf16[64,1024]{1,0:T(8,128)(2,1)} %ts_hbm.1, bf16[64,1024]{1,0:T(8,128)(2,1)} %it_hbm.1, bf16[64,1024]{1,0:T(8,128)(2,1)} %tt_hbm.1), custom_call_target="tpu_custom_call" | custom-call | tf_op jit(solution)/shard_map/pallas_call | solution.py:400
  46.5 1.2 %slice.3 = f32[1,1]{1,0:T(1,128)} slice(f32[8,128]{1,0:T(8,128)} %get-tuple-element.6), slice={[0:1], [0:1]} | slice | bytes 8 | tf_op jit(solution)/shard_map/slice | solution.py:422
  47.7 0.0 copy-start
  47.7 1.7 %copy.9 = f32[64,1024]{1,0:T(8,128)} copy(f32[64,1024]{1,0:T(8,128)} %get-tuple-element.13) | data formatting | bytes 524288
  49.4 0.0 copy-done
  49.4 0.7 %copy.10 = f32[64,1024]{1,0:T(8,128)} copy(f32[64,1024]{1,0:T(8,128)S(1)} %copy-done) | data formatting | bytes 524288
Async XLA Ops:
  47.7 1.7 %copy-start = (f32[64,1024]{1,0:T(8,128)S(1)}, f32[64,1024]{1,0:T(8,128)}, u32[]{:S(2)}) copy-start(f32[64,1024]{1,0:T(8,128)} %get-tuple-element.14) | copy-start | bytes 786436

commit v3 on v2

--- a/solution.py
+++ b/solution.py
@@ -61,7 +61,8 @@
     loss_ref, ig_ref, tg_ref,
     imgs, imgo, imgt, txts, txtt,
     s_ref, t_ref, rowtmp, rstat, cstat, la, lb, gbuf, grecv,
-    pi, inarrow, inear, idirect, ijoint, ifar, pt, tnarrow, tnear, tdirect, tjoint, tfar,
+    pi, inarrow, inear, islim, islims, idirect, ijoint, ifar,
+    pt, tnarrow, tnear, tslim, tslims, tdirect, tjoint, tfar,
     local_sem, send_sem, rimgs, rimgo, rimgt, rtxts, rtxtt, rrow, rcol, rla, rlb, rg,
     rinear, ridirect, rifar, rtnear, rtdirect, rtfar,
 ):
@@ -202,14 +203,7 @@
         forward(*pair)
     collect(*pairs[0])
     s_ref[...] = logit_scale * contract_last(imgs[...], txts[...])
-    collect(*pairs[1])
-    if K > 1:
-        send(imgs, imgo, rimgo, partner)
-    t_ref[...] = logit_scale * contract_last(imgt[...], txtt[...])
-
     rows, width = s_ref.shape
-    col_s = jnp.max(s_ref[...], axis=0, keepdims=True)
-    col_t = jnp.max(t_ref[...], axis=0, keepdims=True)
     lane = lax.broadcasted_iota(jnp.int32, (n, 128), 1)
     col_id = lax.broadcasted_iota(jnp.int32, (1, width), 1)
     col_slot = position(col_id, n, T)
@@ -218,39 +212,48 @@
     slot_h = slot_h - slot_k * H
     col_id = (((slot_h * A + lo) * K + slot_k) * R + slot_r) * n + col_id - col_slot * n
     row_id = lax.broadcasted_iota(jnp.int32, (n, 1), 0)
-    sums = [0.0] * 3
-    diagonal = 0.0
 
     def eye(b):
         base = (r * g["C"] + (hi * A + b) * K + k) * n
         return row_id + base == col_id
 
+    def pack(values, into, index):
+        for i, value in values:
+            into = jnp.where(index == i, value, into)
+        return into
+
+    col_s = jnp.max(s_ref[...], axis=0, keepdims=True)
+    col_total = diagonal = 0.0
+    for b in range(A):
+        at = slice(b * n, (b + 1) * n)
+        s = s_ref[at, :]
+        row_s = jnp.max(s, axis=1, keepdims=True)
+        row_total = jnp.sum(jnp.exp(s - row_s), axis=1, keepdims=True)
+        rowtmp[at, :] = pack(((0, row_s), (1, row_total)), jnp.zeros((n, 128), f32), lane)
+        col_total += jnp.sum(jnp.exp(s - col_s), axis=0, keepdims=True)
+        diagonal += jnp.sum(jnp.where(eye(b), s, 0.0), axis=0, keepdims=True)
+    collect(*pairs[1])
+    if K > 1:
+        send(imgs, imgo, rimgo, partner)
+    t_ref[...] = logit_scale * contract_last(imgt[...], txtt[...])
+
+    col_t = jnp.max(t_ref[...], axis=0, keepdims=True)
+    sums = [0.0] * 2
     for b in range(A):
         at = slice(b * n, (b + 1) * n)
         s, t = s_ref[at, :], t_ref[at, :]
         gap = t - s
-        row_s = jnp.max(s, axis=1, keepdims=True)
         row_t = jnp.max(t, axis=1, keepdims=True)
         row_weight = jnp.exp(t - row_t)
-        stats = (
-            row_s,
-            jnp.sum(jnp.exp(s - row_s), axis=1, keepdims=True),
-            row_t,
-            jnp.sum(row_weight, axis=1, keepdims=True),
-            jnp.sum(row_weight * gap, axis=1, keepdims=True),
-        )
-        packed = jnp.zeros((n, 128), f32)
-        for i, value in enumerate(stats):
-            packed = jnp.where(lane == i, value, packed)
-        rowtmp[at, :] = packed
+        row_sums = [jnp.sum(v, axis=1, keepdims=True) for v in (row_weight, row_weight * gap)]
+        rowtmp[at, :] = pack(((2, row_t), (3, row_sums[0]), (4, row_sums[1])), rowtmp[at, :], lane)
         col_weight = jnp.exp(t - col_t)
-        parts = (jnp.exp(s - col_s), col_weight, col_weight * gap)
-        sums = [old + jnp.sum(new, axis=0, keepdims=True) for old, new in zip(sums, parts)]
-        diagonal += jnp.sum(jnp.where(eye(b), s, 0.0), axis=0, keepdims=True)
+        sums = [
+            old + jnp.sum(new, axis=0, keepdims=True)
+            for old, new in zip(sums, (col_weight, col_weight * gap))
+        ]
     line = lax.broadcasted_iota(jnp.int32, (8, width), 0)
-    packed = jnp.zeros((8, width), f32)
-    for i, value in enumerate((col_s, sums[0], col_t, sums[1], sums[2])):
-        packed = jnp.where(line == i, value, packed)
+    packed = pack(enumerate((col_s, col_total, col_t, *sums)), jnp.zeros((8, width), f32), line)
     cstat[0] = packed
     for e, target in enumerate(b_peers, 1):
         send(cstat.at[0], cstat.at[e], rcol.at[e], target)
@@ -299,27 +302,32 @@
         partial += jnp.dot(gbuf[j], txts[j * half : (j + 1) * half, :], preferred_element_type=f32)
     pi[...] = partial
 
-    def first_hops(part, out_index, in_index, outer, inner, narrow, near, nears, direct, directs, target):
+    def first_hops(part, out_index, in_index, outer, inner, narrow, near, nears, slim, slims, direct, directs, target):
         for j in range(S):
             for do in range(1, outer):
                 for di in range(1, inner):
                     e = (do - 1) * (inner - 1) + di - 1
                     to = up(in_index, di, inner)
-                    send(piece(part, up(out_index, do, outer) * inner + to, j), piece(near, e, j),
-                         nears.at[e, j], target(out_index, to))
+                    src = piece(part, up(out_index, do, outer) * inner + to, j)
+                    if j % 2 == 0:
+                        piece(slims, e, j)[...] = src[...].astype(bf16)
+                        send(piece(slims, e, j), piece(slim, e, j), nears.at[e, j], target(out_index, to))
+                    else:
+                        send(src, piece(near, e, j), nears.at[e, j], target(out_index, to))
         for di in range(1, inner):
             to = up(in_index, di, inner)
             block(narrow, di - 1)[...] = block(part, out_index * inner + to)[...].astype(bf16)
             send(block(narrow, di - 1), block(direct, di - 1), directs.at[di - 1], target(out_index, to))
 
-    def second_hops(part, out_index, in_index, outer, inner, near, nears, joint, far, fars, target, j):
+    def second_hops(part, out_index, in_index, outer, inner, near, nears, slim, joint, far, fars, target, j):
         for do in range(1, outer):
             to = up(out_index, do, outer)
             value = piece(part, to * inner + in_index, j)[...]
             for di in range(1, inner):
                 e = (do - 1) * (inner - 1) + di - 1
-                arrived(piece(near, e, j), nears.at[e, j])
-                value += piece(near, e, j)[...]
+                landed = piece(slim if j % 2 == 0 else near, e, j)
+                arrived(landed, nears.at[e, j])
+                value += landed[...].astype(f32)
             piece(joint, do - 1, j)[...] = value.astype(bf16)
             send(piece(joint, do - 1, j), piece(far, do - 1, j), fars.at[do - 1, j], target(to, in_index))
 
@@ -340,7 +348,7 @@
     def text_target(h_, r_):
         return dev(r_, h_, lo, k)
 
-    first_hops(pi, p, q, PP, Q, inarrow, inear, rinear, idirect, ridirect, image_target)
+    first_hops(pi, p, q, PP, Q, inarrow, inear, rinear, islim, islims, idirect, ridirect, image_target)
 
     if K > 1:
         arrived(imgo, rimgo)
@@ -349,10 +357,10 @@
     if K > 1:
         partial += contract_first(grecv[...], imgo[...])
     pt[...] = partial
-    first_hops(pt, hi, r, H, R, tnarrow, tnear, rtnear, tdirect, rtdirect, text_target)
+    first_hops(pt, hi, r, H, R, tnarrow, tnear, rtnear, tslim, tslims, tdirect, rtdirect, text_target)
     for j in range(S):
-        second_hops(pi, p, q, PP, Q, inear, rinear, ijoint, ifar, rifar, image_target, j)
-        second_hops(pt, hi, r, H, R, tnear, rtnear, tjoint, tfar, rtfar, text_target, j)
+        second_hops(pi, p, q, PP, Q, inear, rinear, islim, ijoint, ifar, rifar, image_target, j)
+        second_hops(pt, hi, r, H, R, tnear, rtnear, tslim, tjoint, tfar, rtfar, text_target, j)
         if j == 0:
             for d in range(1, A):
                 arrived(la.at[d], rla.at[d])
@@ -368,6 +376,16 @@
     for copy in pending:
         copy.wait_send()
     assert len(pending) == n_send, len(pending)
+
+
+def leave(loss_in, image_in, text_in, loss_out, image_out, text_out, sems):
+    image_copy = pltpu.make_async_copy(image_in, image_out, sems.at[0])
+    text_copy = pltpu.make_async_copy(text_in, text_out, sems.at[1])
+    image_copy.start()
+    text_copy.start()
+    loss_out[0, 0] = jnp.max(loss_in[...])
+    image_copy.wait()
+    text_copy.wait()
 
 
 def solution(mesh):
@@ -390,6 +408,7 @@
             near, direct, far = max(near, 1) * n, max(direct, 1) * n, max(far, 1) * n
             return (
                 vmem((size, width), f32), vmem((direct, width), bf16), vmem((near, width), f32),
+                vmem((near, width), bf16), vmem((near, width), bf16),
                 vmem((direct, width), bf16), vmem((far, width), bf16), vmem((far, width), bf16),
             )
 
@@ -399,7 +418,7 @@
         block_out = jax.ShapeDtypeStruct((n, width), f32)
         loss, image_grad, text_grad = pl.pallas_call(
             functools.partial(kernel, g, n_send, total),
-            out_shape=(jax.ShapeDtypeStruct((8, 128), f32), block_out, block_out),
+            out_shape=(vmem((8, 128), f32), vmem((n, width), f32), vmem((n, width), f32)),
             in_specs=[pl.BlockSpec(memory_space=pl.ANY)] * 4,
             out_specs=[pl.BlockSpec(memory_space=pltpu.VMEM)] * 3,
             scratch_shapes=[
@@ -419,6 +438,14 @@
                 collective_id=0, has_side_effects=True, vmem_limit_bytes=56 * 1024 * 1024
             ),
         )(image_student, text_student, image_teacher, text_teacher)
+        loss, image_grad, text_grad = pl.pallas_call(
+            leave,
+            out_shape=(jax.ShapeDtypeStruct((1, 1), f32), block_out, block_out),
+            in_specs=[pl.BlockSpec(memory_space=pltpu.VMEM)] * 3,
+            out_specs=[pl.BlockSpec(memory_space=pltpu.SMEM)] + [pl.BlockSpec(memory_space=pl.ANY)] * 2,
+            scratch_shapes=[dma((2,))],
+            compiler_params=pltpu.CompilerParams(vmem_limit_bytes=1024 * 1024),
+        )(loss, image_grad, text_grad)
         return loss[0, 0], image_grad, text_grad
 
     return jax.shard_map(

time: 50.3 us -> 46.5 us (0.924)
  local copies, waits for them, and re-layouts: 3.61 us -> 0 us
    unnamed x4 -> x0, local copies, waits for them, and re-layouts: 2.42 us -> none
    slice x1 -> x0, local copies, waits for them, and re-layouts: 1.19 us -> none  [body(): return (loss[0, 0], image_grad, text_grad)]
    pallas_call x1 -> x2, Pallas kernels: 45.9 us -> 45.7 us  [the longest x1 44.4 us: body(): pl.pallas_call(functools.partial(kernel, g, n_send, total), out_shape=(vm...]
where the time goes in v3:
time: 46.5 us; the launch traced here: 46.4 us
  Pallas kernels  45.7 us (98%)
  between operations  0.64 us (1%)
    pallas_call x1, Pallas kernels, body(): pl.pallas_call(functools.partial(kernel, g, n_send, total), out_shape=(vm...  44.4 us
    pallas_call x1, Pallas kernels, body(): pl.pallas_call(leave, out_shape=(jax.ShapeDtypeStruct((1, 1), f32), block...  1.32 us

profile of v3, /device:TPU:0, one launch (start us, length us, event | category | flops | bytes accessed | tf_op | source)
XLA Modules:
  0.0 46.4 jit_solution(11787144496688941443)
XLA Ops:
  0.6 44.4 %shard_map.67 = (f32[8,128]{1,0:T(8,128)S(1)}, f32[64,1024]{1,0:T(8,128)S(1)}, f32[64,1024]{1,0:T(8,128)S(1)}) custom-call(bf16[64,1024]{1,0:T(8,128)(2,1)} %is_hbm.1, bf16[64,1024]{1,0:T(8,128)(2,1)} %ts_hbm.1, bf16[64,1024]{1,0:T(8,128)(2,1)} %it_hbm.1, bf16[64,1024]{1,0:T(8,128)(2,1)} %tt_hbm.1), custom_call_target="tpu_custom_call" | custom-call | tf_op jit(solution)/shard_map/pallas_call | solution.py:419
  45.1 1.3 %shard_map.68 = (f32[1,1]{1,0:T(1,128)}, f32[64,1024]{1,0:T(8,128)}, f32[64,1024]{1,0:T(8,128)}) custom-call(f32[8,128]{1,0:T(8,128)S(1)} %get-tuple-element.9.loss_in, f32[64,1024]{1,0:T(8,128)S(1)} %get-tuple-element.10.image_in, f32[64,1024]{1,0:T(8,128)S(1)} %get-tuple-element.11.text_in), custom_call_target="tpu_custom_call" | custom-call | tf_op jit(solution)/shard_map/pallas_call | solution.py:441

commit v4 on v3

--- a/solution.py
+++ b/solution.py
@@ -302,14 +302,26 @@
         partial += jnp.dot(gbuf[j], txts[j * half : (j + 1) * half, :], preferred_element_type=f32)
     pi[...] = partial
 
-    def first_hops(part, out_index, in_index, outer, inner, narrow, near, nears, slim, slims, direct, directs, target):
-        for j in range(S):
+    def first_hops(part, out_index, in_index, outer, inner, narrow, near, nears, slim, slims, direct, directs, joint, far, fars, target):
+        for do in range(1, outer):
+            there = up(out_index, do, outer)
+            for di in range(inner):
+                to = up(in_index, di, inner)
+                value = piece(part, there * inner + to, 0)[...].astype(bf16)
+                if di == 0:
+                    src, dst, sem = piece(joint, do - 1, 0), piece(far, do - 1, 0), fars.at[do - 1, 0]
+                else:
+                    e = (do - 1) * (inner - 1) + di - 1
+                    src, dst, sem = piece(slims, e, 0), piece(slim, e, 0), nears.at[e, 0]
+                src[...] = value
+                send(src, dst, sem, target(there, to))
+        for j in range(1, S):
             for do in range(1, outer):
                 for di in range(1, inner):
                     e = (do - 1) * (inner - 1) + di - 1
                     to = up(in_index, di, inner)
                     src = piece(part, up(out_index, do, outer) * inner + to, j)
-                    if j % 2 == 0:
+                    if j % 2:
                         piece(slims, e, j)[...] = src[...].astype(bf16)
                         send(piece(slims, e, j), piece(slim, e, j), nears.at[e, j], target(out_index, to))
                     else:
@@ -325,13 +337,13 @@
             value = piece(part, to * inner + in_index, j)[...]
             for di in range(1, inner):
                 e = (do - 1) * (inner - 1) + di - 1
-                landed = piece(slim if j % 2 == 0 else near, e, j)
+                landed = piece(slim if j % 2 else near, e, j)
                 arrived(landed, nears.at[e, j])
                 value += landed[...].astype(f32)
             piece(joint, do - 1, j)[...] = value.astype(bf16)
             send(piece(joint, do - 1, j), piece(far, do - 1, j), fars.at[do - 1, j], target(to, in_index))
 
-    def last_sum(part, out_index, in_index, outer, inner, direct, directs, far, fars):
+    def last_sum(out_ref, part, out_index, in_index, outer, inner, slim, nears, direct, directs, far, fars):
         value = block(part, out_index * inner + in_index)[...]
         for di in range(1, inner):
             arrived(block(direct, di - 1), directs.at[di - 1])
@@ -340,7 +352,10 @@
             for j in range(S):
                 arrived(piece(far, do - 1, j), fars.at[do - 1, j])
             value += block(far, do - 1)[...].astype(f32)
-        return logit_scale * value
+        out_ref[...] = logit_scale * value
+        for e in range((outer - 1) * (inner - 1)):
+            arrived(piece(slim, e, 0), nears.at[e, 0])
+            out_ref[:m, :] += logit_scale * piece(slim, e, 0)[...].astype(f32)
 
     def image_target(p_, q_):
         return dev(r, hi, p_ * Q + q_, k)
@@ -348,7 +363,7 @@
     def text_target(h_, r_):
         return dev(r_, h_, lo, k)
 
-    first_hops(pi, p, q, PP, Q, inarrow, inear, rinear, islim, islims, idirect, ridirect, image_target)
+    first_hops(pi, p, q, PP, Q, inarrow, inear, rinear, islim, islims, idirect, ridirect, ijoint, ifar, rifar, image_target)
 
     if K > 1:
         arrived(imgo, rimgo)
@@ -357,22 +372,26 @@
     if K > 1:
         partial += contract_first(grecv[...], imgo[...])
     pt[...] = partial
-    first_hops(pt, hi, r, H, R, tnarrow, tnear, rtnear, tslim, tslims, tdirect, rtdirect, text_target)
-    for j in range(S):
+    first_hops(pt, hi, r, H, R, tnarrow, tnear, rtnear, tslim, tslims, tdirect, rtdirect, tjoint, tfar, rtfar, text_target)
+    def loss_round():
+        for d in range(1, A):
+            arrived(la.at[d], rla.at[d])
+        lb[0] = functools.reduce(jnp.add, [la[d] for d in range(A)])
+        for e, target in enumerate(b_peers, 1):
+            send(lb.at[0], lb.at[e], rlb.at[e], target)
+
+    for j in range(1, S):
         second_hops(pi, p, q, PP, Q, inear, rinear, islim, ijoint, ifar, rifar, image_target, j)
         second_hops(pt, hi, r, H, R, tnear, rtnear, tslim, tjoint, tfar, rtfar, text_target, j)
-        if j == 0:
-            for d in range(1, A):
-                arrived(la.at[d], rla.at[d])
-            lb[0] = functools.reduce(jnp.add, [la[d] for d in range(A)])
-            for e, target in enumerate(b_peers, 1):
-                send(lb.at[0], lb.at[e], rlb.at[e], target)
-
+        if j == 1:
+            loss_round()
+    if S == 1:
+        loss_round()
     for e in range(1, T):
         arrived(lb.at[e], rlb.at[e])
     loss_ref[...] = functools.reduce(jnp.add, [lb[e] for e in range(T)]) / total
-    ig_ref[...] = last_sum(pi, p, q, PP, Q, idirect, ridirect, ifar, rifar)
-    tg_ref[...] = last_sum(pt, hi, r, H, R, tdirect, rtdirect, tfar, rtfar)
+    last_sum(ig_ref, pi, p, q, PP, Q, islim, rinear, idirect, ridirect, ifar, rifar)
+    last_sum(tg_ref, pt, hi, r, H, R, tslim, rtnear, tdirect, rtdirect, tfar, rtfar)
     for copy in pending:
         copy.wait_send()
     assert len(pending) == n_send, len(pending)

time: 46.5 us -> 44.4 us (0.955)
  Pallas kernels: 45.7 us -> 43.6 us
    pallas_call x1, Pallas kernels: 44.4 us -> 42.3 us  [body(): pl.pallas_call(functools.partial(kernel, g, n_send, total), out_shape=(vm...]
where the time goes in v4:
time: 44.4 us; the launch traced here: 44.2 us
  Pallas kernels  43.6 us (98%)
  between operations  0.64 us (1%)
    pallas_call x1, Pallas kernels, body(): pl.pallas_call(functools.partial(kernel, g, n_send, total), out_shape=(vm...  42.3 us
    pallas_call x1, Pallas kernels, body(): pl.pallas_call(leave, out_shape=(jax.ShapeDtypeStruct((1, 1), f32), block...  1.32 us

profile of v4, /device:TPU:0, one launch (start us, length us, event | category | flops | bytes accessed | tf_op | source)
XLA Modules:
  0.0 44.2 jit_solution(3374275698371001529)
XLA Ops:
  0.6 42.3 %shard_map.67 = (f32[8,128]{1,0:T(8,128)S(1)}, f32[64,1024]{1,0:T(8,128)S(1)}, f32[64,1024]{1,0:T(8,128)S(1)}) custom-call(bf16[64,1024]{1,0:T(8,128)(2,1)} %is_hbm.1, bf16[64,1024]{1,0:T(8,128)(2,1)} %ts_hbm.1, bf16[64,1024]{1,0:T(8,128)(2,1)} %it_hbm.1, bf16[64,1024]{1,0:T(8,128)(2,1)} %tt_hbm.1), custom_call_target="tpu_custom_call" | custom-call | tf_op jit(solution)/shard_map/pallas_call | solution.py:438
  42.9 1.3 %shard_map.68 = (f32[1,1]{1,0:T(1,128)}, f32[64,1024]{1,0:T(8,128)}, f32[64,1024]{1,0:T(8,128)}) custom-call(f32[8,128]{1,0:T(8,128)S(1)} %get-tuple-element.9.loss_in, f32[64,1024]{1,0:T(8,128)S(1)} %get-tuple-element.10.image_in, f32[64,1024]{1,0:T(8,128)S(1)} %get-tuple-element.11.text_in), custom_call_target="tpu_custom_call" | custom-call | tf_op jit(solution)/shard_map/pallas_call | solution.py:460

commit v5 on v4

--- a/solution.py
+++ b/solution.py
@@ -365,13 +365,11 @@
 
     first_hops(pi, p, q, PP, Q, inarrow, inear, rinear, islim, islims, idirect, ridirect, ijoint, ifar, rifar, image_target)
 
+    pt[...] = contract_first(gbuf[k], imgs[...])
     if K > 1:
         arrived(imgo, rimgo)
         arrived(grecv, rg)
-    partial = contract_first(gbuf[k], imgs[...])
-    if K > 1:
-        partial += contract_first(grecv[...], imgo[...])
-    pt[...] = partial
+        pt[...] += contract_first(grecv[...], imgo[...])
     first_hops(pt, hi, r, H, R, tnarrow, tnear, rtnear, tslim, tslims, tdirect, rtdirect, tjoint, tfar, rtfar, text_target)
     def loss_round():
         for d in range(1, A):

time: 44.4 us -> 45 us (1.014)
  Pallas kernels: 43.6 us -> 44.2 us
    pallas_call x1, Pallas kernels: 42.3 us -> 42.9 us  [body(): pl.pallas_call(functools.partial(kernel, g, n_send, total), out_shape=(vm...]
where the time goes in v5:
time: 45 us; the launch traced here: 44.8 us
  Pallas kernels  44.2 us (98%)
  between operations  0.64 us (1%)
    pallas_call x1, Pallas kernels, body(): pl.pallas_call(functools.partial(kernel, g, n_send, total), out_shape=(vm...  42.9 us
    pallas_call x1, Pallas kernels, body(): pl.pallas_call(leave, out_shape=(jax.ShapeDtypeStruct((1, 1), f32), block...  1.32 us

profile of v5, /device:TPU:0, one launch (start us, length us, event | category | flops | bytes accessed | tf_op | source)
XLA Modules:
  0.0 44.8 jit_solution(9666368079449773084)
XLA Ops:
  0.6 42.9 %shard_map.67 = (f32[8,128]{1,0:T(8,128)S(1)}, f32[64,1024]{1,0:T(8,128)S(1)}, f32[64,1024]{1,0:T(8,128)S(1)}) custom-call(bf16[64,1024]{1,0:T(8,128)(2,1)} %is_hbm.1, bf16[64,1024]{1,0:T(8,128)(2,1)} %ts_hbm.1, bf16[64,1024]{1,0:T(8,128)(2,1)} %it_hbm.1, bf16[64,1024]{1,0:T(8,128)(2,1)} %tt_hbm.1), custom_call_target="tpu_custom_call" | custom-call | tf_op jit(solution)/shard_map/pallas_call | solution.py:436
  43.5 1.3 %shard_map.68 = (f32[1,1]{1,0:T(1,128)}, f32[64,1024]{1,0:T(8,128)}, f32[64,1024]{1,0:T(8,128)}) custom-call(f32[8,128]{1,0:T(8,128)S(1)} %get-tuple-element.9.loss_in, f32[64,1024]{1,0:T(8,128)S(1)} %get-tuple-element.10.image_in, f32[64,1024]{1,0:T(8,128)S(1)} %get-tuple-element.11.text_in), custom_call_target="tpu_custom_call" | custom-call | tf_op jit(solution)/shard_map/pallas_call | solution.py:458
